TPU v7x, 32 devices: a whole 2x2x4 slice. The times are simulated.
32 devices in a mesh: freq: 4 (over y, x), band: 8 (over z, core).
Axes of the slice: x: 2, y: 2, z: 4, core: 2. Of those that a mesh axis runs over, the one named last changes fastest.
Arguments:
- pair_density: bfloat16 [1024, 2, 8192], P(('freq', 'band')), may hold values from -6 to 6
- trial_vectors: bfloat16 [16, 2, 64, 8192], P('freq', None, None, 'band'), may hold values from -6 to 6
- frequency: float32 [16], P('freq'), may hold values from 0.05 to 20
- val_energy: float32 [32], replicated, may hold values from -3 to -0.1
- cond_energy: float32 [32], replicated, may hold values from 0.1 to 4
- pair_index: int32 [1024], P(('freq', 'band')), may hold values from 0 to 1023, each once
Outputs:
- images: float32 [16, 2, 64, 8192], P('freq', None, None, 'band')
- subspace: float32 [16, 2, 64, 64], P('freq')
Inputs may be any that keep to these rules, and one draw needn't show every extreme that they name: `pair_index`: every pair number 0 to 1023 appears exactly once.
All inputs are finite; a program needn't handle non-finite values.
Results may differ from a plain program's by a relative error of at most 0.0085.
Values may be sent and summed in bfloat16 or wider, within the bound.
No kernel may reach another device: no remote copies, remote signals or barrier semaphores. Data moves between devices by JAX's collectives and lax.ppermute only.
A program may use at most 128 MiB of HBM per device.

v0:
```python
import math
import jax
import jax.numpy as jnp
from jax import lax
from jax.sharding import PartitionSpec as P


def local_weights(pair_index, frequency, val_energy, cond_energy, prefactor):
    cond_count = cond_energy.shape[0]
    val_count = val_energy.shape[0]
    cond_pick = jnp.sum(
        jnp.where(
            (pair_index % cond_count)[:, None] == jnp.arange(cond_count)[None, :],
            cond_energy[None, :],
            0.0,
        ),
        axis=1,
    )
    val_pick = jnp.sum(
        jnp.where(
            (pair_index // cond_count)[:, None] == jnp.arange(val_count)[None, :],
            val_energy[None, :],
            0.0,
        ),
        axis=1,
    )
    delta = cond_pick - val_pick
    ratio = delta[:, None] / (
        delta[:, None] * delta[:, None] + frequency[None, :] * frequency[None, :]
    )
    return (-4.0 * prefactor * ratio).astype(jnp.bfloat16)


def crossing_terms(density, vectors):
    products = jnp.einsum("pcg,fekg->fcekp", density, vectors, preferred_element_type=jnp.float32)
    return jnp.stack(
        [products[:, 0, 0] + products[:, 1, 1], products[:, 0, 1] - products[:, 1, 0]], 1
    )


def scale_terms(crossings, weights):
    factor = jnp.transpose(weights.astype(jnp.float32))[:, None, None, :]
    return (factor * crossings).astype(jnp.bfloat16)


def mix_terms(scaled):
    scaled_real = scaled[:, 0]
    scaled_imag = scaled[:, 1]
    return jnp.stack(
        [jnp.stack([scaled_real, -scaled_imag], 1), jnp.stack([scaled_imag, scaled_real], 1)], 1
    )


def image_terms(density, mixed):
    return jnp.einsum("pcg,fdckp->fdkg", density, mixed, preferred_element_type=jnp.float32)


def shards(pair_density, trial_vectors, frequency, val_energy, cond_energy, pair_index):
    groups = lax.axis_size("freq")
    members = lax.axis_size("band")
    pair_count = pair_density.shape[0] * groups * members
    grid_count = trial_vectors.shape[3] * members
    prefactor = 1.0 / math.sqrt(2.0 * grid_count * pair_count)
    regrouped = lax.all_to_all(pair_density, "band", split_axis=2, concat_axis=0, tiled=True)
    grouped = lax.all_gather(regrouped, "freq", axis=0, tiled=True)
    all_index = lax.all_gather(pair_index, ("freq", "band"), axis=0, tiled=True)
    crossings = crossing_terms(grouped, trial_vectors)
    summed = lax.psum(crossings, "band")
    all_weights = local_weights(all_index, frequency, val_energy, cond_energy, prefactor)
    scaled = scale_terms(summed, all_weights)
    images = image_terms(grouped, mix_terms(scaled))
    vectors = trial_vectors.astype(jnp.float32)
    highest = lax.Precision.HIGHEST
    real_part = jnp.einsum(
        "fkg,flg->fkl", vectors[:, 0], images[:, 0], precision=highest
    ) + jnp.einsum("fkg,flg->fkl", vectors[:, 1], images[:, 1], precision=highest)
    imag_part = jnp.einsum(
        "fkg,flg->fkl", vectors[:, 0], images[:, 1], precision=highest
    ) - jnp.einsum("fkg,flg->fkl", vectors[:, 1], images[:, 0], precision=highest)
    partial_value = jnp.stack([real_part, imag_part], 1) / grid_count
    subspace = lax.psum(partial_value, "band")
    return (images, subspace)


def solution(mesh):
    return jax.shard_map(
        shards,
        mesh=mesh,
        in_specs=(
            P(("freq", "band"), None, None),
            P("freq", None, None, "band"),
            P("freq"),
            P(),
            P(),
            P(("freq", "band")),
        ),
        out_specs=(P("freq", None, None, "band"), P("freq", None, None, None)),
        check_vma=False,
    )
```

profile of v0, /device:TPU:0, one launch (start us, length us, event | category | flops | bytes accessed | tf_op | source)
XLA Modules:
  0.0 269.7 jit_solution(9058504637230988360)
XLA Ops:
  7.2 0.0 all-gather.2.cloned.1.call-start
  7.2 10.8 %copy.31 = bf16[32,2,8192]{0,1,2:T(2,128)(2,1)} copy(bf16[32,2,8192]{2,1,0:T(2,128)(2,1)} %param.6) | data formatting | bytes 2097152 | tf_op args[0]
  18.0 7.0 %reshape.101 = bf16[8,2,32768]{2,1,0:T(2,128)(2,1)S(1)} reshape(bf16[8192,2,32]{2,1,0:T(2,128)(2,1)} %bitcast.76) | data formatting | bytes 2097152
  24.9 32.7 %all_to_all.18 = bf16[8,2,32768]{2,1,0:T(2,128)(2,1)S(1)} all-to-all(bf16[8,2,32768]{2,1,0:T(2,128)(2,1)S(1)} %reshape.101), channel_id=1, replica_groups=mesh['freq'=4,'band'=8] {'band'}, dimensions={0} | all-to-all | bytes 2097152 | tf_op jit(solution)/shard_map/all_to_all | solution.py:64
  57.7 4.5 %reshape.102 = bf16[8192,2,32]{2,1,0:T(2,128)(2,1)} reshape(bf16[8,2,32768]{2,1,0:T(2,128)(2,1)S(1)} %all_to_all.18) | data formatting | bytes 2097152
  62.2 0.0 copy-start.1
  62.2 10.5 %copy.32 = bf16[32,2,8,1024]{3,0,2,1:T(8,128)(2,1)} copy(bf16[32,2,8,1024]{0,1,3,2:T(2,128)(2,1)} %bitcast.75) | data formatting | bytes 2097152 | tf_op jit(solution)/shard_map/all_to_all | solution.py:64
  72.6 0.0 all-gather.2.cloned.1.call-update
  72.6 0.0 all-reduce.4.cloned.1.call-start
  72.7 51.6 %all-gather.2.cloned.1.call-done = bf16[1024,2,1024]{2,0,1:T(8,128)(2,1)} async-done(((bf16[256,2,1024]{2,0,1:T(8,128)(2,1)}), bf16[1024,2,1024]{2,0,1:T(8,128)(2,1)}) %all-gather.2.cloned.1.call-update) | async-done | bytes 4194320 | tf_op jit(solution)/shard_map/all_gather | solution.py:65
  124.3 0.0 copy-done.1
  124.3 4.6 %fusion.4 = f32[4,2,2,64,1024]{4,3,1,2,0:T(8,128)S(1)} fusion(bf16[1024,2,1024]{2,0,1:T(8,128)(2,1)} %all-gather.2.cloned.1.call-done, bf16[4,2,64,1024]{3,2,1,0:T(8,128)(2,1)S(1)} %copy-done.1), kind=kOutput, calls=%fused_computation.4 | convolution fusion | flops 2147483648 | bytes 9437184 | tf_op jit(solution)/shard_map/pcg,fekg->fcekp/dot_general | solution.py:35
  128.9 0.1 fusion.15
  129.0 0.1 fusion.17
  129.2 1.5 pad_maximum_fusion
  130.6 0.0 copy-start.5
  130.6 0.0 copy-start.6
  130.6 0.0 copy-start.2
  130.6 0.0 copy-start.3
  130.6 0.0 all-reduce.4.cloned.1.call-update
  130.7 0.0 all-reduce.6.cloned.1.call-start
  130.7 0.6 copy-done.5
  131.3 0.0 copy-done.6
  131.3 0.2 dynamic-update-slice
  131.5 39.6 %all-reduce = s32[1024]{0:T(1024)S(1)} all-reduce(s32[1024]{0:T(1024)S(1)} %dynamic-update-slice), channel_id=1, replica_groups=mesh['freq'=4,'band'=8] {'freq','band'}, use_global_device_ids=true, to_apply=%add | all-reduce | flops 1024 | bytes 8192
  171.2 0.0 copy-done.2
  171.2 0.0 copy-done.3
  171.2 0.1 select_reduce_fusion
  171.3 0.1 fusion.29
  171.4 25.1 %all-reduce.4.cloned.1.call-done = f32[4,2,64,1024]{3,2,0,1:T(8,128)} async-done(((f32[4,2,64,1024]{3,2,0,1:T(8,128)}), f32[4,2,64,1024]{3,2,0,1:T(8,128)}) %all-reduce.4.cloned.1.call-update) | async-done | bytes 2097168 | tf_op jit(solution)/shard_map/psum | solution.py:68
  196.5 1.8 multiply_convert_fusion
  198.4 0.0 copy-start.4
  198.4 0.1 slice_negate_fusion
  198.5 0.2 maximum_bitcast_fusion
  198.7 1.9 copy-done.4
  200.5 2.3 fusion.8
  202.9 0.0 copy-start
  202.9 0.6 fusion.20
  203.5 0.6 fusion.19
  204.2 0.6 fusion.13
  204.8 0.0 copy-done
  204.8 0.6 fusion.14
  205.4 0.7 maximum_multiply_fusion
  206.2 0.0 all-reduce.6.cloned.1.call-update
  206.2 55.2 %all-reduce.6.cloned.1.call-done = f32[4,2,64,64]{2,3,0,1:T(8,128)} async-done(((f32[4,2,64,64]{2,3,0,1:T(8,128)}), f32[4,2,64,64]{2,3,0,1:T(8,128)}) %all-reduce.6.cloned.1.call-update) | async-done | bytes 131088 | tf_op jit(solution)/shard_map/psum | solution.py:81
  261.4 1.8 copy.38
  (4 shorter events, 0.0 us)
Async XLA Ops:
  7.2 117.1 %all-gather.2.cloned.1.call-start = ((), (), s32[]{:S(2)}) async-start(), calls=%async_computation.1 | async-start | bytes 5242880 | tf_op jit(solution)/shard_map/all_gather | solution.py:65
  62.2 62.2 %copy-start.1 = (bf16[4,2,64,1024]{3,2,1,0:T(8,128)(2,1)S(1)}, bf16[4,2,64,1024]{3,2,1,0:T(8,128)(2,1)}, u32[]{:S(2)}) copy-start(bf16[4,2,64,1024]{3,2,1,0:T(8,128)(2,1)} %param.7) | copy-start | bytes 3145732
  72.6 123.9 %all-reduce.4.cloned.1.call-start = ((), (), s32[]{:S(2)}) async-start(), calls=%async_computation.2 | async-start | bytes 4194304 | tf_op jit(solution)/shard_map/psum | solution.py:68
  130.6 0.7 copy-start.5
  130.6 0.7 copy-start.6
  130.6 40.6 %copy-start.2 = (f32[32]{0:T(128)S(1)}, f32[32]{0:T(128)}, u32[]{:S(2)}) copy-start(f32[32]{0:T(128)} %param.9) | copy-start | bytes 388
  130.6 40.6 %copy-start.3 = (f32[32]{0:T(128)S(1)}, f32[32]{0:T(128)}, u32[]{:S(2)}) copy-start(f32[32]{0:T(128)} %param.10) | copy-start | bytes 388
  130.7 130.8 %all-reduce.6.cloned.1.call-start = ((), (), s32[]{:S(2)}) async-start(), calls=%async_computation.3 | async-start | bytes 524288 | tf_op jit(solution)/shard_map/psum | solution.py:81
  198.4 2.2 copy-start.4
  202.9 1.9 copy-start
Sparse Core Ops, SparseCore 0:
  72.8 51.4 all-gather.1
  130.8 65.6 all-reduce.3
  206.3 55.0 all-reduce.5
where the time goes:
time: 271 us; the launch traced here: 270 us
  waiting for transfers between devices  132 us (49%)
  blocking collectives  72.4 us (27%)
  local copies, waits for them, and re-layouts  37.2 us (14%)
  between operations  13.9 us (5%)
  matrix products  9.4 us (3%)
  other arithmetic  4.8 us (2%)
    psum x1, waiting for transfers between devices, shards(): subspace = lax.psum(partial_value, 'band')  55.2 us
    all_gather x1, waiting for transfers between devices, shards(): grouped = lax.all_gather(regrouped, 'freq', axis=0, tiled=True)  51.6 us
    unnamed x1, blocking collectives  39.6 us
    all_to_all x1, blocking collectives, shards(): lax.all_to_all(pair_density, 'band', split_axis=2, concat_axis=0, tiled=T...  32.7 us
    unnamed x20, local copies, waits for them, and re-layouts  26.7 us
    psum x1, waiting for transfers between devices, shards(): summed = lax.psum(crossings, 'band')  25.1 us
    all_to_all x1, local copies, waits for them, and re-layouts, shards(): lax.all_to_all(pair_density, 'band', split_axis=2, concat_axis=0, tiled=T...  10.5 us
  transfers between devices with their start and end apart: 3, of which 3 were waited for; matrix products, arithmetic and copies ran while one was open for 0% of the time, Pallas kernels for 0%

commit v1 on v0

--- a/solution.py
+++ b/solution.py
@@ -3,6 +3,17 @@
 import jax.numpy as jnp
 from jax import lax
 from jax.sharding import PartitionSpec as P
+
+
+def in_blocks(x, dim, size):
+    before, after = (x.shape[:dim], x.shape[dim + 1 :])
+    return jnp.moveaxis(x.reshape(*before, size, -1, *after), dim, 0)
+
+
+def joined_along(pieces, dim):
+    pieces = jnp.moveaxis(pieces, 0, dim)
+    shape = pieces.shape
+    return pieces.reshape(*shape[:dim], shape[dim] * shape[dim + 1], *shape[dim + 2 :])
 
 
 def local_weights(pair_index, frequency, val_energy, cond_energy, prefactor):
@@ -61,7 +72,14 @@
     pair_count = pair_density.shape[0] * groups * members
     grid_count = trial_vectors.shape[3] * members
     prefactor = 1.0 / math.sqrt(2.0 * grid_count * pair_count)
-    regrouped = lax.all_to_all(pair_density, "band", split_axis=2, concat_axis=0, tiled=True)
+    size, index = (lax.axis_size("band"), lax.axis_index("band"))
+    blocks = in_blocks(pair_density, 2, size)
+    outs = [blocks[index]]
+    for turn in range(1, size):
+        sent = blocks[index ^ turn]
+        outs.append(lax.ppermute(sent, "band", [(i, i ^ turn) for i in range(size)]))
+    blocks = jnp.stack(outs)[index ^ jnp.arange(size)]
+    regrouped = joined_along(blocks, 0)
     grouped = lax.all_gather(regrouped, "freq", axis=0, tiled=True)
     all_index = lax.all_gather(pair_index, ("freq", "band"), axis=0, tiled=True)
     crossings = crossing_terms(grouped, trial_vectors)

time: 271 us -> 242 us (0.89)
  blocking collectives: 72.4 us -> 40.1 us
  local copies, waits for them, and re-layouts: 37.2 us -> 11.1 us
  waiting for transfers between devices: 132 us -> 152 us
  starting transfers between devices: 0.12 us -> 10.2 us
    all_to_all x1 -> x0, blocking collectives: 32.7 us -> none  [shards(): lax.all_to_all(pair_density, 'band', split_axis=2, concat_axis=0, tiled=T...]
    unnamed x20 -> x31, local copies, waits for them, and re-layouts: 26.7 us -> 5.18 us
    ppermute x0 -> x7, waiting for transfers between devices: none -> 13.6 us  [shards(): lax.ppermute(sent, 'band', [(i, i ^ turn) for i in range(size)])]
    all_to_all x1 -> x0, local copies, waits for them, and re-layouts: 10.5 us -> none  [shards(): lax.all_to_all(pair_density, 'band', split_axis=2, concat_axis=0, tiled=T...]
    ppermute x0 -> x7, starting transfers between devices: none -> 10 us  [shards(): lax.ppermute(sent, 'band', [(i, i ^ turn) for i in range(size)])]
    all_gather x1, waiting for transfers between devices: 51.6 us -> 58.3 us  [shards(): grouped = lax.all_gather(regrouped, 'freq', axis=0, tiled=True)]
  transfers between devices with their start and end apart: 3 -> 10, of which waited for: 3 -> 5; matrix products, arithmetic and copies ran while one was open for 0% -> 0% of each run, Pallas kernels for 0% -> 0%
where the time goes in v1:
time: 242 us
  waiting for transfers between devices  152 us (63%)
  blocking collectives  40.1 us (17%)
  between operations  14.1 us (6%)
  local copies, waits for them, and re-layouts  11.1 us (5%)
  starting transfers between devices  10.2 us (4%)
  matrix products  9.4 us (4%)
  other arithmetic  4.92 us (2%)
    all_gather x1, waiting for transfers between devices, shards(): grouped = lax.all_gather(regrouped, 'freq', axis=0, tiled=True)  58.3 us
    psum x1, waiting for transfers between devices, shards(): subspace = lax.psum(partial_value, 'band')  55.2 us
    unnamed x1, blocking collectives  40.1 us
    psum x1, waiting for transfers between devices, shards(): summed = lax.psum(crossings, 'band')  24.7 us
    ppermute x7, waiting for transfers between devices, shards(): lax.ppermute(sent, 'band', [(i, i ^ turn) for i in range(size)])  13.6 us
    ppermute x7, starting transfers between devices, shards(): lax.ppermute(sent, 'band', [(i, i ^ turn) for i in range(size)])  10 us
    unnamed x31, local copies, waits for them, and re-layouts  5.18 us
  transfers between devices with their start and end apart: 10, of which 5 were waited for; matrix products, arithmetic and copies ran while one was open for 0% of the time, Pallas kernels for 0%

profile of v1, /device:TPU:0, one launch (start us, length us, event | category | flops | bytes accessed | tf_op | source)
XLA Modules:
  0.0 241.6 jit_solution(8619679413355077814)
XLA Ops:
  7.2 0.0 all-gather.2.cloned.1.call-start
  7.2 1.8 reshape.148
  9.1 2.4 constant_dynamic-slice_fusion
  11.5 0.1 copy.105
  11.6 0.6 collective-permute-start
  12.2 0.1 copy.104
  12.2 2.6 %collective-permute-start.1 = (bf16[32,2,1024]{2,0,1:T(8,128)(2,1)S(1)}, bf16[32,2,1024]{2,0,1:T(8,128)(2,1)S(1)}, u32[]{:S(2)}, u32[]{:S(2)}) collective-permute-start(bf16[32,2,1024]{2,0,1:T(8,128)(2,1)S(1)} %bitcast.125), channel_id=1, source_target_pairs={{0,2},{1,3},{2,0},{3,1},{4,6},{5,7},{6,4},{7,5},{8,10},{9,11},{10,... | collective-permute-start | bytes 393224 | tf_op jit(solution)/shard_map/ppermute | solution.py:80
  14.9 0.1 copy.103
  15.0 0.2 collective-permute-start.2
  15.1 0.1 copy.102
  15.2 2.8 %collective-permute-start.3 = (bf16[32,2,1024]{2,0,1:T(8,128)(2,1)S(1)}, bf16[32,2,1024]{2,0,1:T(8,128)(2,1)S(1)}, u32[]{:S(2)}, u32[]{:S(2)}) collective-permute-start(bf16[32,2,1024]{2,0,1:T(8,128)(2,1)S(1)} %bitcast.122), channel_id=1, source_target_pairs={{0,4},{1,5},{2,6},{3,7},{4,0},{5,1},{6,2},{7,3},{8,12},{9,13},{10,... | collective-permute-start | bytes 393224 | tf_op jit(solution)/shard_map/ppermute | solution.py:80
  18.0 0.1 copy.101
  18.1 0.1 collective-permute-start.4
  18.2 0.1 fusion.29
  18.3 0.1 copy.100
  18.4 0.1 copy.99
  18.5 0.0 collective-permute-done
  18.5 3.6 %collective-permute-start.5 = (bf16[32,2,1024]{2,0,1:T(8,128)(2,1)S(1)}, bf16[32,2,1024]{2,0,1:T(8,128)(2,1)S(1)}, u32[]{:S(2)}, u32[]{:S(2)}) collective-permute-start(bf16[32,2,1024]{2,0,1:T(8,128)(2,1)S(1)} %bitcast.124), channel_id=1, source_target_pairs={{0,6},{1,7},{2,4},{3,5},{4,2},{5,3},{6,0},{7,1},{8,14},{9,15},{10,... | collective-permute-start | bytes 393224 | tf_op jit(solution)/shard_map/ppermute | solution.py:80
  22.1 0.0 collective-permute-done.1
  22.1 0.2 collective-permute-start.6
  22.3 4.2 %collective-permute-done.2 = bf16[32,2,1024]{2,0,1:T(8,128)(2,1)S(1)} collective-permute-done((bf16[32,2,1024]{2,0,1:T(8,128)(2,1)S(1)}, bf16[32,2,1024]{2,0,1:T(8,128)(2,1)S(1)}, u32[]{:S(2)}, u32[]{:S(2)}) %collective-permute-start.2) | collective-permute-done | bytes 131104 | tf_op jit(solution)/shard_map/ppermute | solution.py:80
  26.5 0.0 collective-permute-done.3
  26.6 9.3 %collective-permute-done.4 = bf16[32,2,1024]{2,0,1:T(8,128)(2,1)S(1)} collective-permute-done((bf16[32,2,1024]{2,0,1:T(8,128)(2,1)S(1)}, bf16[32,2,1024]{2,0,1:T(8,128)(2,1)S(1)}, u32[]{:S(2)}, u32[]{:S(2)}) %collective-permute-start.4) | collective-permute-done | bytes 131104 | tf_op jit(solution)/shard_map/ppermute | solution.py:80
  35.9 0.0 collective-permute-done.5
  35.9 0.0 collective-permute-done.6
  36.0 0.6 gather_fusion
  36.6 0.0 copy-start.1
  36.6 1.1 copy.30
  37.7 0.0 all-gather.2.cloned.1.call-update
  37.7 0.0 all-reduce.4.cloned.1.call-start
  37.8 58.3 %all-gather.2.cloned.1.call-done = bf16[1024,2,1024]{2,0,1:T(8,128)(2,1)} async-done(((bf16[256,2,1024]{2,0,1:T(8,128)(2,1)}), bf16[1024,2,1024]{2,0,1:T(8,128)(2,1)}) %all-gather.2.cloned.1.call-update) | async-done | bytes 4194320 | tf_op jit(solution)/shard_map/all_gather | solution.py:83
  96.0 0.0 copy-done.1
  96.0 4.6 %fusion.4 = f32[4,2,2,64,1024]{4,3,2,0,1:T(8,128)S(1)} fusion(bf16[1024,2,1024]{2,0,1:T(8,128)(2,1)} %all-gather.2.cloned.1.call-done, bf16[4,2,64,1024]{3,2,1,0:T(8,128)(2,1)S(1)} %copy-done.1), kind=kOutput, calls=%fused_computation.5 | convolution fusion | flops 2147483648 | bytes 9437184 | tf_op jit(solution)/shard_map/pcg,fekg->fcekp/dot_general | solution.py:46
  100.6 0.1 fusion.15
  100.7 0.2 fusion.17
  100.9 1.5 pad_maximum_fusion
  102.5 0.0 copy-start.5
  102.5 0.0 all-reduce.4.cloned.1.call-update
  102.5 0.0 all-reduce.6.cloned.1.call-start
  102.5 0.6 copy-done.5
  103.1 0.0 copy-done.6
  103.1 0.2 dynamic-update-slice
  103.4 40.1 %all-reduce = s32[1024]{0:T(1024)S(1)} all-reduce(s32[1024]{0:T(1024)S(1)} %dynamic-update-slice), channel_id=1, replica_groups=mesh['freq'=4,'band'=8] {'freq','band'}, use_global_device_ids=true, to_apply=%add | all-reduce | flops 1024 | bytes 8192
  143.4 0.0 copy-done.2
  143.5 0.0 copy-done.3
  143.5 0.1 select_reduce_fusion
  143.6 0.1 fusion.30
  143.7 24.7 %all-reduce.4.cloned.1.call-done = f32[4,2,64,1024]{3,2,0,1:T(8,128)} async-done(((f32[4,2,64,1024]{3,2,0,1:T(8,128)}), f32[4,2,64,1024]{3,2,0,1:T(8,128)}) %all-reduce.4.cloned.1.call-update) | async-done | bytes 2097168 | tf_op jit(solution)/shard_map/psum | solution.py:86
  168.4 1.8 multiply_convert_fusion
  170.3 0.0 copy-start.4
  170.3 0.1 slice_negate_fusion
  170.4 0.2 maximum_bitcast_fusion
  170.6 1.9 copy-done.4
  172.4 2.3 fusion.8
  174.8 0.0 copy-start
  174.8 0.6 fusion.19
  175.4 0.6 fusion.20
  176.1 0.6 fusion.14
  176.7 0.0 copy-done
  176.7 0.6 fusion.13
  177.3 0.7 maximum_multiply_fusion
  178.1 0.0 all-reduce.6.cloned.1.call-update
  178.1 55.2 %all-reduce.6.cloned.1.call-done = f32[4,2,64,64]{2,3,0,1:T(8,128)} async-done(((f32[4,2,64,64]{2,3,0,1:T(8,128)}), f32[4,2,64,64]{2,3,0,1:T(8,128)}) %all-reduce.6.cloned.1.call-update) | async-done | bytes 131088 | tf_op jit(solution)/shard_map/psum | solution.py:99
  233.3 1.8 copy.36
  (16 shorter events, 0.1 us)
Async XLA Ops:
  7.2 88.9 %all-gather.2.cloned.1.call-start = ((), (), s32[]{:S(2)}) async-start(), calls=%async_computation | async-start | bytes 5242880 | tf_op jit(solution)/shard_map/all_gather | solution.py:83
  11.6 6.9 %collective-permute-start = (bf16[32,2,1024]{2,0,1:T(8,128)(2,1)S(1)}, bf16[32,2,1024]{2,0,1:T(8,128)(2,1)S(1)}, u32[]{:S(2)}, u32[]{:S(2)}) collective-permute-start(bf16[32,2,1024]{2,0,1:T(8,128)(2,1)S(1)} %bitcast.126), channel_id=1, source_target_pairs={{0,1},{1,0},{2,3},{3,2},{4,5},{5,4},{6,7},{7,6},{8,9},{9,8},{10,11... | collective-permute-start | bytes 393224 | tf_op jit(solution)/shard_map/ppermute | solution.py:80
  12.2 9.9 %collective-permute-start.1 = (bf16[32,2,1024]{2,0,1:T(8,128)(2,1)S(1)}, bf16[32,2,1024]{2,0,1:T(8,128)(2,1)S(1)}, u32[]{:S(2)}, u32[]{:S(2)}) collective-permute-start(bf16[32,2,1024]{2,0,1:T(8,128)(2,1)S(1)} %bitcast.125), channel_id=1, source_target_pairs={{0,2},{1,3},{2,0},{3,1},{4,6},{5,7},{6,4},{7,5},{8,10},{9,11},{10,... | collective-permute-start | bytes 393224 | tf_op jit(solution)/shard_map/ppermute | solution.py:80
  15.0 11.6 %collective-permute-start.2 = (bf16[32,2,1024]{2,0,1:T(8,128)(2,1)S(1)}, bf16[32,2,1024]{2,0,1:T(8,128)(2,1)S(1)}, u32[]{:S(2)}, u32[]{:S(2)}) collective-permute-start(bf16[32,2,1024]{2,0,1:T(8,128)(2,1)S(1)} %bitcast.123), channel_id=1, source_target_pairs={{0,3},{1,2},{2,1},{3,0},{4,7},{5,6},{6,5},{7,4},{8,11},{9,10},{10,... | collective-permute-start | bytes 393224 | tf_op jit(solution)/shard_map/ppermute | solution.py:80
  15.2 11.3 %collective-permute-start.3 = (bf16[32,2,1024]{2,0,1:T(8,128)(2,1)S(1)}, bf16[32,2,1024]{2,0,1:T(8,128)(2,1)S(1)}, u32[]{:S(2)}, u32[]{:S(2)}) collective-permute-start(bf16[32,2,1024]{2,0,1:T(8,128)(2,1)S(1)} %bitcast.122), channel_id=1, source_target_pairs={{0,4},{1,5},{2,6},{3,7},{4,0},{5,1},{6,2},{7,3},{8,12},{9,13},{10,... | collective-permute-start | bytes 393224 | tf_op jit(solution)/shard_map/ppermute | solution.py:80
  18.1 17.8 %collective-permute-start.4 = (bf16[32,2,1024]{2,0,1:T(8,128)(2,1)S(1)}, bf16[32,2,1024]{2,0,1:T(8,128)(2,1)S(1)}, u32[]{:S(2)}, u32[]{:S(2)}) collective-permute-start(bf16[32,2,1024]{2,0,1:T(8,128)(2,1)S(1)} %bitcast.121), channel_id=1, source_target_pairs={{0,5},{1,4},{2,7},{3,6},{4,1},{5,0},{6,3},{7,2},{8,13},{9,12},{10,... | collective-permute-start | bytes 393224 | tf_op jit(solution)/shard_map/ppermute | solution.py:80
  18.5 17.4 %collective-permute-start.5 = (bf16[32,2,1024]{2,0,1:T(8,128)(2,1)S(1)}, bf16[32,2,1024]{2,0,1:T(8,128)(2,1)S(1)}, u32[]{:S(2)}, u32[]{:S(2)}) collective-permute-start(bf16[32,2,1024]{2,0,1:T(8,128)(2,1)S(1)} %bitcast.124), channel_id=1, source_target_pairs={{0,6},{1,7},{2,4},{3,5},{4,2},{5,3},{6,0},{7,1},{8,14},{9,15},{10,... | collective-permute-start | bytes 393224 | tf_op jit(solution)/shard_map/ppermute | solution.py:80
  22.1 13.8 %collective-permute-start.6 = (bf16[32,2,1024]{2,0,1:T(8,128)(2,1)S(1)}, bf16[32,2,1024]{2,0,1:T(8,128)(2,1)S(1)}, u32[]{:S(2)}, u32[]{:S(2)}) collective-permute-start(bf16[32,2,1024]{2,0,1:T(8,128)(2,1)S(1)} %bitcast.120), channel_id=1, source_target_pairs={{0,7},{1,6},{2,5},{3,4},{4,3},{5,2},{6,1},{7,0},{8,15},{9,14},{10,... | collective-permute-start | bytes 393224 | tf_op jit(solution)/shard_map/ppermute | solution.py:80
  36.6 59.4 %copy-start.1 = (bf16[4,2,64,1024]{3,2,1,0:T(8,128)(2,1)S(1)}, bf16[4,2,64,1024]{3,2,1,0:T(8,128)(2,1)}, u32[]{:S(2)}) copy-start(bf16[4,2,64,1024]{3,2,1,0:T(8,128)(2,1)} %param.7) | copy-start | bytes 3145732
  37.7 130.7 %all-reduce.4.cloned.1.call-start = ((), (), s32[]{:S(2)}) async-start(), calls=%async_computation.1 | async-start | bytes 4194304 | tf_op jit(solution)/shard_map/psum | solution.py:86
  102.5 0.7 copy-start.5
  102.5 0.7 copy-start.6
  102.5 41.0 %copy-start.2 = (f32[32]{0:T(128)S(1)}, f32[32]{0:T(128)}, u32[]{:S(2)}) copy-start(f32[32]{0:T(128)} %param.9) | copy-start | bytes 388
  102.5 41.0 %copy-start.3 = (f32[32]{0:T(128)S(1)}, f32[32]{0:T(128)}, u32[]{:S(2)}) copy-start(f32[32]{0:T(128)} %param.10) | copy-start | bytes 388
  102.5 130.8 %all-reduce.6.cloned.1.call-start = ((), (), s32[]{:S(2)}) async-start(), calls=%async_computation.2 | async-start | bytes 524288 | tf_op jit(solution)/shard_map/psum | solution.py:99
  170.3 2.2 copy-start.4
  174.8 1.9 copy-start
Sparse Core Ops, SparseCore 0:
  37.8 58.1 all-gather.1
  102.6 65.7 all-reduce.3
  178.2 55.0 all-reduce.5
